TPU v7x, 128 devices: a whole 4x4x4 slice. The times are simulated.
128 devices in a mesh: seq: 32 (over z, x, core), group: 4 (over y).
Axes of the slice: x: 4, y: 4, z: 4, core: 2. Of those that a mesh axis runs over, the one named last changes fastest.
Arguments:
- new_queries: bfloat16 [32, 8, 8, 128], P('seq', 'group'), may hold values from -6 to 6
- stored_keys: bfloat16 [32, 8, 16384, 128], P(None, 'group', 'seq'), may hold values from -6 to 6
- stored_values: bfloat16 [32, 8, 16384, 128], P(None, 'group', 'seq'), may hold values from -6 to 6
- used_length: int32 [32], replicated, may hold values from 8192 to 16384
- out_weight: bfloat16 [8, 8, 128, 5120], P('group'), may hold values from -0.0625 to 0.0625
Outputs:
- token_out: bfloat16 [32, 5120], P('seq', 'group')
All inputs are finite; a program needn't handle non-finite values.
Results may differ from a plain program's by a relative error of at most 0.0025.
Values may be sent and summed in bfloat16 or wider, within the bound.
No kernel may reach another device: no remote copies, remote signals or barrier semaphores. Data moves between devices by JAX's collectives and lax.ppermute only.
A program may use at most 128 MiB of HBM per device.

v0:
```python
import jax
import jax.numpy as jnp
from jax import lax
from jax.sharding import PartitionSpec as P

HEAD_SIZE = 128


def per_device(new_queries, stored_keys, stored_values, used_length, out_weight):
    all_queries = lax.all_gather(new_queries, "seq", axis=0, tiled=True)
    logit = jnp.einsum(
        "bkgd,bktd->bkgt", all_queries, stored_keys, preferred_element_type=jnp.float32
    ) * HEAD_SIZE ** (-0.5)
    positions = lax.axis_index("seq") * stored_keys.shape[2] + jnp.arange(stored_keys.shape[2])
    filled = positions[None, :] < used_length[:, None]
    logit = jnp.where(filled[:, None, None, :], logit, -1e30)
    top = jnp.max(logit, axis=-1)
    part = jnp.where(filled[:, None, None, :], jnp.exp(logit - top[..., None]), 0.0)
    weight_sum = jnp.sum(part, axis=-1)
    read_sum = jnp.einsum(
        "bkgt,bktd->bkgd", part, stored_values.astype(jnp.float32), precision=lax.Precision.HIGHEST
    )
    tops, sums, parts = (
        lax.all_to_all(top[None], "seq", split_axis=1, concat_axis=0, tiled=True),
        lax.all_to_all(weight_sum[None], "seq", split_axis=1, concat_axis=0, tiled=True),
        lax.all_to_all(read_sum[None], "seq", split_axis=1, concat_axis=0, tiled=True),
    )
    best = jnp.max(tops, axis=0)
    scale = jnp.exp(tops - best)
    weight_own = jnp.sum(sums * scale, axis=0)
    read_own = jnp.sum(parts * scale[..., None], axis=0)
    read = (read_own / weight_own[..., None]).astype(jnp.bfloat16)
    term = jnp.einsum("bkgd,kgdm->bm", read, out_weight, preferred_element_type=jnp.float32)
    token_out = lax.psum_scatter(term, "group", scatter_dimension=1, tiled=True).astype(
        jnp.bfloat16
    )
    return token_out


def solution(mesh):
    in_specs = (
        P("seq", "group", None, None),
        P(None, "group", "seq", None),
        P(None, "group", "seq", None),
        P(),
        P("group", None, None, None),
    )
    out_specs = P("seq", "group")
    return jax.shard_map(
        per_device, mesh=mesh, in_specs=in_specs, out_specs=out_specs, check_vma=False
    )
```

profile of v0, /device:TPU:1, one launch (start us, length us, event | category | flops | bytes accessed | tf_op | source)
XLA Modules:
  0.0 134.0 jit_solution(4825849419178507323)
XLA Ops:
  6.5 27.3 %all_gather.3 = bf16[32,2,8,128]{3,2,1,0:T(8,128)(2,1)S(1)} all-gather(bf16[1,2,8,128]{3,2,1,0:T(8,128)(2,1)} %param.5), channel_id=1, replica_groups=mesh['seq'=32,'group'=4] {'seq'}, dimensions={0}, use_global_device_ids=true | all-gather | bytes 135168 | tf_op jit(solution)/shard_map/all_gather | solution.py:10
  33.9 0.7 broadcast_compare_fusion
  34.6 6.4 %fusion.18 = (f32[32,2,8]{2,1,0:T(2,128)}, f32[32,2,8,512]{3,2,1,0:T(8,128)S(1)}) fusion(bf16[32,2,8,128]{3,2,1,0:T(8,128)(2,1)S(1)} %all_gather.3, bf16[32,2,512,128]{3,2,1,0:T(8,128)(2,1)} %param.6, pred[32,512]{1,0:T(8,128)(4,1)S(1)} %broadcast_compare_fusion), kind=kOutput, calls=%fused_computation.25 | convolution fusion | flops 67894784 | bytes 9586688 | tf_op jit(solution)/shard_map/bkgd,bktd->bkgt/dot_general | solution.py:11
  41.0 4.9 %all-to-all-start.1 = ((f32[1,32,2,8]{3,2,0,1:T(2,128)}), f32[1,32,2,8]{3,2,0,1:T(2,128)S(1)}, u32[]{:S(2)}, u32[]{:S(2)}) async-start(f32[1,32,2,8]{3,2,0,1:T(2,128)} %bitcast.3), calls=%async_computation.1 | async-start | bytes 65536 | tf_op jit(solution)/shard_map/all_to_all | solution.py:24
  45.9 1.8 %fusion.6 = f32[32,2,8]{2,1,0:T(2,128)} fusion(f32[32,2,8,512]{3,2,1,0:T(8,128)S(1)} %get-tuple-element.6, f32[32,2,8]{2,1,0:T(2,128)} %get-tuple-element.5, pred[32,512]{1,0:T(8,128)(4,1)S(1)} %broadcast_compare_fusion), kind=kLoop, calls=%fused_computation.7 | loop fusion | flops 785920 | bytes 1069056 | tf_op jit(solution)/shard_map/reduce_sum | solution.py:19
  47.6 5.5 %all-to-all-done.1 = f32[1,32,2,8]{3,2,0,1:T(2,128)S(1)} async-done(((f32[1,32,2,8]{3,2,0,1:T(2,128)}), f32[1,32,2,8]{3,2,0,1:T(2,128)S(1)}, u32[]{:S(2)}, u32[]{:S(2)}) %all-to-all-start.1) | async-done | bytes 2080 | tf_op jit(solution)/shard_map/all_to_all | solution.py:24
  53.1 3.9 %all-to-all-start.2 = ((f32[1,32,2,8]{3,2,0,1:T(2,128)}), f32[1,32,2,8]{3,2,0,1:T(2,128)S(1)}, u32[]{:S(2)}, u32[]{:S(2)}) async-start(f32[1,32,2,8]{3,2,0,1:T(2,128)} %bitcast.5), calls=%async_computation.2 | async-start | bytes 65536 | tf_op jit(solution)/shard_map/all_to_all | solution.py:25
  57.0 6.5 %convolution_bitcast_fusion = f32[1,32,2,8,128]{4,3,2,0,1:T(8,128)} fusion(bf16[32,2,512,128]{3,2,1,0:T(8,128)(2,1)} %param.7, f32[32,2,8,512]{3,2,1,0:T(8,128)S(1)} %get-tuple-element.6, f32[32,2,8]{2,1,0:T(2,128)} %get-tuple-element.5, pred[32,512]{1,0:T(8,128)(4,1)S(1)} %broadcast_compare_fusion), kind=kOutput, calls=%fused_computation.5 | convolution fusion | flops 403177472 | bytes 9717760 | tf_op jit(solution)/shard_map/bkgt,bktd->bkgd/dot_general | solution.py:20
  63.6 0.8 all-to-all-done.2
  64.4 6.7 %all-to-all-start = ((f32[1,32,2,8,128]{4,3,2,0,1:T(8,128)}), f32[1,32,2,8,128]{4,3,2,0,1:T(8,128)S(1)}, u32[]{:S(2)}, u32[]{:S(2)}) async-start(f32[1,32,2,8,128]{4,3,2,0,1:T(8,128)} %convolution_bitcast_fusion), calls=%async_computation | async-start | bytes 524288 | tf_op jit(solution)/shard_map/all_to_all | solution.py:26
  71.1 0.0 reduce-scatter.4.cloned.1.call-start
  71.1 0.1 fusion.14
  71.2 8.7 %all-to-all-done = f32[1,32,2,8,128]{4,3,2,0,1:T(8,128)S(1)} async-done(((f32[1,32,2,8,128]{4,3,2,0,1:T(8,128)}), f32[1,32,2,8,128]{4,3,2,0,1:T(8,128)S(1)}, u32[]{:S(2)}, u32[]{:S(2)}) %all-to-all-start) | async-done | bytes 262176 | tf_op jit(solution)/shard_map/all_to_all | solution.py:26
  80.0 0.1 fusion.10
  80.1 0.1 fusion.16
  80.2 13.4 %fusion.2 = f32[5120,1]{1,0:T(8,128)} fusion(bf16[2,8,128,5120]{3,2,1,0:T(8,128)(2,1)} %param.9, bf16[2,8,128,1]{2,1,0,3:T(8,128)(2,1)S(1)} %fusion.16), kind=kOutput, calls=%fused_computation.2 | convolution fusion | flops 20971520 | bytes 20996096 | tf_op jit(solution)/shard_map/bkgd,kgdm->bm/dot_general | solution.py:33
  93.6 0.0 reduce-scatter.4.cloned.1.call-update
  93.6 31.6 %reduce-scatter.4.cloned.1.call-done = f32[1280,1]{1,0:T(8,128)} async-done(((f32[5120,1]{1,0:T(8,128)}), f32[1280,1]{1,0:T(8,128)}) %reduce-scatter.4.cloned.1.call-update) | async-done | bytes 5136
  125.3 1.9 %copy.11 = bf16[1,1280]{1,0:T(2,128)(2,1)} copy(f32[1,1280]{0,1:T(8,128)} %bitcast.41) | data formatting | bytes 7680
  (3 shorter events, 0.1 us)
Async XLA Ops:
  41.0 12.2 %all-to-all-start.1 = ((f32[1,32,2,8]{3,2,0,1:T(2,128)}), f32[1,32,2,8]{3,2,0,1:T(2,128)S(1)}, u32[]{:S(2)}, u32[]{:S(2)}) async-start(f32[1,32,2,8]{3,2,0,1:T(2,128)} %bitcast.3), calls=%async_computation.1 | async-start | bytes 65536 | tf_op jit(solution)/shard_map/all_to_all | solution.py:24
  53.1 11.3 %all-to-all-start.2 = ((f32[1,32,2,8]{3,2,0,1:T(2,128)}), f32[1,32,2,8]{3,2,0,1:T(2,128)S(1)}, u32[]{:S(2)}, u32[]{:S(2)}) async-start(f32[1,32,2,8]{3,2,0,1:T(2,128)} %bitcast.5), calls=%async_computation.2 | async-start | bytes 65536 | tf_op jit(solution)/shard_map/all_to_all | solution.py:25
  64.4 15.6 %all-to-all-start = ((f32[1,32,2,8,128]{4,3,2,0,1:T(8,128)}), f32[1,32,2,8,128]{4,3,2,0,1:T(8,128)S(1)}, u32[]{:S(2)}, u32[]{:S(2)}) async-start(f32[1,32,2,8,128]{4,3,2,0,1:T(8,128)} %convolution_bitcast_fusion), calls=%async_computation | async-start | bytes 524288 | tf_op jit(solution)/shard_map/all_to_all | solution.py:26
  71.1 54.2 %reduce-scatter.4.cloned.1.call-start = ((), (), s32[]{:S(2)}) async-start(), calls=%async_computation.4 | async-start | bytes 3276800
Sparse Core Ops, SparseCore 0:
  93.8 31.4 reduce-scatter.3
where the time goes:
time: 135 us; the launch traced here: 134 us
  waiting for transfers between devices  46.7 us (35%)
  blocking collectives  27.3 us (20%)
  matrix products  26.3 us (19%)
  starting transfers between devices  15.5 us (11%)
  between operations  13.4 us (10%)
  other arithmetic  2.83 us (2%)
  local copies, waits for them, and re-layouts  1.91 us (1%)
    unnamed x2, waiting for transfers between devices  31.6 us
    all_gather x1, blocking collectives, per_device(): all_queries = lax.all_gather(new_queries, 'seq', axis=0, tiled=True)  27.3 us
    dot_general x1, matrix products, per_device(): jnp.einsum('bkgd,kgdm->bm', read, out_weight, preferred_element_type=jnp....  13.4 us
    all_to_all x1, waiting for transfers between devices, per_device(): lax.all_to_all(read_sum[None], 'seq', split_axis=1, concat_axis=0, tiled=...  8.74 us
    all_to_all x1, starting transfers between devices, per_device(): lax.all_to_all(read_sum[None], 'seq', split_axis=1, concat_axis=0, tiled=...  6.68 us
    dot_general x1, matrix products, per_device(): jnp.einsum('bkgt,bktd->bkgd', part, stored_values.astype(jnp.float32), pr...  6.5 us
    dot_general x1, matrix products, per_device(): jnp.einsum('bkgd,bktd->bkgt', all_queries, stored_keys, preferred_element...  6.36 us
    all_to_all x1, waiting for transfers between devices, per_device(): lax.all_to_all(top[None], 'seq', split_axis=1, concat_axis=0, tiled=True)  5.49 us
  transfers between devices with their start and end apart: 4, of which 4 were waited for; matrix products, arithmetic and copies ran while one was open for 6% of the time, Pallas kernels for 0%

commit v1 on v0

--- a/solution.py
+++ b/solution.py
@@ -7,7 +7,8 @@
 
 
 def per_device(new_queries, stored_keys, stored_values, used_length, out_weight):
-    all_queries = lax.all_gather(new_queries, "seq", axis=0, tiled=True)
+    copies = jnp.concatenate([new_queries] * lax.axis_size("seq"), axis=0)
+    all_queries = lax.all_to_all(copies, "seq", 0, 0, tiled=True)
     logit = jnp.einsum(
         "bkgd,bktd->bkgt", all_queries, stored_keys, preferred_element_type=jnp.float32
     ) * HEAD_SIZE ** (-0.5)

time: 135 us -> 124 us (0.919)
  blocking collectives: 27.3 us -> 0 us
  starting transfers between devices: 15.5 us -> 23.9 us
  waiting for transfers between devices: 46.7 us -> 53.7 us
    all_gather x1 -> x0, blocking collectives: 27.3 us -> none  [per_device(): all_queries = lax.all_gather(new_queries, 'seq', axis=0, tiled=True)]
    all_to_all x0 -> x1, starting transfers between devices: none -> 9.42 us  [per_device(): all_queries = lax.all_to_all(copies, 'seq', 0, 0, tiled=True)]
    all_to_all x0 -> x1, waiting for transfers between devices: none -> 6.84 us  [per_device(): all_queries = lax.all_to_all(copies, 'seq', 0, 0, tiled=True)]
  transfers between devices with their start and end apart: 4 -> 5, of which waited for: 4 -> 5; matrix products, arithmetic and copies ran while one was open for 6% -> 7% of each run, Pallas kernels for 0% -> 0%
where the time goes in v1:
time: 124 us; the launch traced here: 123 us
  waiting for transfers between devices  53.7 us (43%)
  matrix products  26.3 us (21%)
  starting transfers between devices  23.9 us (19%)
  between operations  13.5 us (11%)
  local copies, waits for them, and re-layouts  3.25 us (3%)
  other arithmetic  2.84 us (2%)
    unnamed x2, waiting for transfers between devices  31.6 us
    dot_general x1, matrix products, per_device(): jnp.einsum('bkgd,kgdm->bm', read, out_weight, preferred_element_type=jnp....  13.4 us
    all_to_all x1, starting transfers between devices, per_device(): all_queries = lax.all_to_all(copies, 'seq', 0, 0, tiled=True)  9.42 us
    all_to_all x1, waiting for transfers between devices, per_device(): lax.all_to_all(read_sum[None], 'seq', split_axis=1, concat_axis=0, tiled=...  8.74 us
    all_to_all x1, waiting for transfers between devices, per_device(): all_queries = lax.all_to_all(copies, 'seq', 0, 0, tiled=True)  6.84 us
    all_to_all x1, starting transfers between devices, per_device(): lax.all_to_all(read_sum[None], 'seq', split_axis=1, concat_axis=0, tiled=...  6.69 us
    dot_general x1, matrix products, per_device(): jnp.einsum('bkgt,bktd->bkgd', part, stored_values.astype(jnp.float32), pr...  6.5 us
    dot_general x1, matrix products, per_device(): jnp.einsum('bkgd,bktd->bkgt', all_queries, stored_keys, preferred_element...  6.36 us
  transfers between devices with their start and end apart: 5, of which 5 were waited for; matrix products, arithmetic and copies ran while one was open for 7% of the time, Pallas kernels for 0%

profile of v1, /device:TPU:1, one launch (start us, length us, event | category | flops | bytes accessed | tf_op | source)
XLA Modules:
  0.0 123.4 jit_solution(7740491030624859670)
XLA Ops:
  6.5 1.3 %concatenate.3 = bf16[32,2,8,128]{3,2,1,0:T(8,128)(2,1)} broadcast(bf16[2,8,128]{2,1,0:T(8,128)(2,1)} %bitcast.43), dimensions={1,2,3} | broadcast | bytes 135168 | tf_op jit(solution)/shard_map/concatenate | solution.py:10
  7.9 9.4 %all-to-all-start = ((bf16[32,2,8,128]{3,2,1,0:T(8,128)(2,1)}), bf16[32,2,8,128]{3,2,1,0:T(8,128)(2,1)S(1)}, u32[]{:S(2)}, u32[]{:S(2)}) async-start(bf16[32,2,8,128]{3,2,1,0:T(8,128)(2,1)} %concatenate.3), calls=%async_computation | async-start | bytes 262144 | tf_op jit(solution)/shard_map/all_to_all | solution.py:11
  17.3 0.7 broadcast_compare_fusion
  18.1 6.8 %all-to-all-done = bf16[32,2,8,128]{3,2,1,0:T(8,128)(2,1)S(1)} async-done(((bf16[32,2,8,128]{3,2,1,0:T(8,128)(2,1)}), bf16[32,2,8,128]{3,2,1,0:T(8,128)(2,1)S(1)}, u32[]{:S(2)}, u32[]{:S(2)}) %all-to-all-start) | async-done | bytes 131104 | tf_op jit(solution)/shard_map/all_to_all | solution.py:11
  24.9 6.4 %fusion.18 = (f32[32,2,8]{2,1,0:T(2,128)}, f32[32,2,8,512]{3,2,1,0:T(8,128)S(1)}) fusion(bf16[32,2,8,128]{3,2,1,0:T(8,128)(2,1)S(1)} %all-to-all-done, bf16[32,2,512,128]{3,2,1,0:T(8,128)(2,1)} %param.6, pred[32,512]{1,0:T(8,128)(4,1)S(1)} %broadcast_compare_fusion), kind=kOutput, calls=%fused_computation.25 | convolution fusion | flops 67894784 | bytes 9586688 | tf_op jit(solution)/shard_map/bkgd,bktd->bkgt/dot_general | solution.py:12
  31.3 3.9 %all-to-all-start.2 = ((f32[1,32,2,8]{3,2,0,1:T(2,128)}), f32[1,32,2,8]{3,2,0,1:T(2,128)S(1)}, u32[]{:S(2)}, u32[]{:S(2)}) async-start(f32[1,32,2,8]{3,2,0,1:T(2,128)} %bitcast.4), calls=%async_computation.2 | async-start | bytes 65536 | tf_op jit(solution)/shard_map/all_to_all | solution.py:25
  35.2 1.8 %fusion.6 = f32[32,2,8]{2,1,0:T(2,128)} fusion(f32[32,2,8,512]{3,2,1,0:T(8,128)S(1)} %get-tuple-element.6, f32[32,2,8]{2,1,0:T(2,128)} %get-tuple-element.5, pred[32,512]{1,0:T(8,128)(4,1)S(1)} %broadcast_compare_fusion), kind=kLoop, calls=%fused_computation.7 | loop fusion | flops 785920 | bytes 1069056 | tf_op jit(solution)/shard_map/reduce_sum | solution.py:20
  36.9 5.6 %all-to-all-done.2 = f32[1,32,2,8]{3,2,0,1:T(2,128)S(1)} async-done(((f32[1,32,2,8]{3,2,0,1:T(2,128)}), f32[1,32,2,8]{3,2,0,1:T(2,128)S(1)}, u32[]{:S(2)}, u32[]{:S(2)}) %all-to-all-start.2) | async-done | bytes 2080 | tf_op jit(solution)/shard_map/all_to_all | solution.py:25
  42.5 3.9 %all-to-all-start.3 = ((f32[1,32,2,8]{3,2,0,1:T(2,128)}), f32[1,32,2,8]{3,2,0,1:T(2,128)S(1)}, u32[]{:S(2)}, u32[]{:S(2)}) async-start(f32[1,32,2,8]{3,2,0,1:T(2,128)} %bitcast.6), calls=%async_computation.3 | async-start | bytes 65536 | tf_op jit(solution)/shard_map/all_to_all | solution.py:26
  46.4 6.5 %convolution_bitcast_fusion = f32[1,32,2,8,128]{4,3,2,0,1:T(8,128)} fusion(bf16[32,2,512,128]{3,2,1,0:T(8,128)(2,1)} %param.7, f32[32,2,8,512]{3,2,1,0:T(8,128)S(1)} %get-tuple-element.6, f32[32,2,8]{2,1,0:T(2,128)} %get-tuple-element.5, pred[32,512]{1,0:T(8,128)(4,1)S(1)} %broadcast_compare_fusion), kind=kOutput, calls=%fused_computation.5 | convolution fusion | flops 403177472 | bytes 9717760 | tf_op jit(solution)/shard_map/bkgt,bktd->bkgd/dot_general | solution.py:21
  53.0 0.8 all-to-all-done.3
  53.8 6.7 %all-to-all-start.1 = ((f32[1,32,2,8,128]{4,3,2,0,1:T(8,128)}), f32[1,32,2,8,128]{4,3,2,0,1:T(8,128)S(1)}, u32[]{:S(2)}, u32[]{:S(2)}) async-start(f32[1,32,2,8,128]{4,3,2,0,1:T(8,128)} %convolution_bitcast_fusion), calls=%async_computation.1 | async-start | bytes 524288 | tf_op jit(solution)/shard_map/all_to_all | solution.py:27
  60.5 0.0 reduce-scatter.4.cloned.1.call-start
  60.5 0.1 fusion.14
  60.6 8.7 %all-to-all-done.1 = f32[1,32,2,8,128]{4,3,2,0,1:T(8,128)S(1)} async-done(((f32[1,32,2,8,128]{4,3,2,0,1:T(8,128)}), f32[1,32,2,8,128]{4,3,2,0,1:T(8,128)S(1)}, u32[]{:S(2)}, u32[]{:S(2)}) %all-to-all-start.1) | async-done | bytes 262176 | tf_op jit(solution)/shard_map/all_to_all | solution.py:27
  69.4 0.1 fusion.10
  69.5 0.1 fusion.16
  69.6 13.4 %fusion.2 = f32[5120,1]{1,0:T(8,128)} fusion(bf16[2,8,128,5120]{3,2,1,0:T(8,128)(2,1)} %param.9, bf16[2,8,128,1]{2,1,0,3:T(8,128)(2,1)S(1)} %fusion.16), kind=kOutput, calls=%fused_computation.2 | convolution fusion | flops 20971520 | bytes 20996096 | tf_op jit(solution)/shard_map/bkgd,kgdm->bm/dot_general | solution.py:34
  83.0 0.0 reduce-scatter.4.cloned.1.call-update
  83.0 31.6 %reduce-scatter.4.cloned.1.call-done = f32[1280,1]{1,0:T(8,128)} async-done(((f32[5120,1]{1,0:T(8,128)}), f32[1280,1]{1,0:T(8,128)}) %reduce-scatter.4.cloned.1.call-update) | async-done | bytes 5136
  114.7 1.9 %copy.11 = bf16[1,1280]{1,0:T(2,128)(2,1)} copy(f32[1,1280]{0,1:T(8,128)} %bitcast.42) | data formatting | bytes 7680
  (3 shorter events, 0.1 us)
Async XLA Ops:
  7.9 17.0 %all-to-all-start = ((bf16[32,2,8,128]{3,2,1,0:T(8,128)(2,1)}), bf16[32,2,8,128]{3,2,1,0:T(8,128)(2,1)S(1)}, u32[]{:S(2)}, u32[]{:S(2)}) async-start(bf16[32,2,8,128]{3,2,1,0:T(8,128)(2,1)} %concatenate.3), calls=%async_computation | async-start | bytes 262144 | tf_op jit(solution)/shard_map/all_to_all | solution.py:11
  31.3 11.3 %all-to-all-start.2 = ((f32[1,32,2,8]{3,2,0,1:T(2,128)}), f32[1,32,2,8]{3,2,0,1:T(2,128)S(1)}, u32[]{:S(2)}, u32[]{:S(2)}) async-start(f32[1,32,2,8]{3,2,0,1:T(2,128)} %bitcast.4), calls=%async_computation.2 | async-start | bytes 65536 | tf_op jit(solution)/shard_map/all_to_all | solution.py:25
  42.5 11.3 %all-to-all-start.3 = ((f32[1,32,2,8]{3,2,0,1:T(2,128)}), f32[1,32,2,8]{3,2,0,1:T(2,128)S(1)}, u32[]{:S(2)}, u32[]{:S(2)}) async-start(f32[1,32,2,8]{3,2,0,1:T(2,128)} %bitcast.6), calls=%async_computation.3 | async-start | bytes 65536 | tf_op jit(solution)/shard_map/all_to_all | solution.py:26
  53.8 15.6 %all-to-all-start.1 = ((f32[1,32,2,8,128]{4,3,2,0,1:T(8,128)}), f32[1,32,2,8,128]{4,3,2,0,1:T(8,128)S(1)}, u32[]{:S(2)}, u32[]{:S(2)}) async-start(f32[1,32,2,8,128]{4,3,2,0,1:T(8,128)} %convolution_bitcast_fusion), calls=%async_computation.1 | async-start | bytes 524288 | tf_op jit(solution)/shard_map/all_to_all | solution.py:27
  60.5 54.2 %reduce-scatter.4.cloned.1.call-start = ((), (), s32[]{:S(2)}) async-start(), calls=%async_computation.5 | async-start | bytes 3276800
Sparse Core Ops, SparseCore 0:
  83.2 31.4 reduce-scatter.3
